TPU v7x, 32 devices: a whole 2x2x4 slice. The times are simulated.
32 devices in a mesh: grp: 2 (over x), col: 8 (over z, core), lay: 2 (over y).
Axes of the slice: x: 2, y: 2, z: 4, core: 2. Of those that a mesh axis runs over, the one named last changes fastest.
Arguments:
- gradient: float32 [2, 2, 24, 6144, 128], P('grp', 'lay', None, 'col'), may hold values from -410 to 410
- momentum: float32 [2, 2, 24, 6144, 128], P('grp', 'lay', None, 'col'), may hold values from -820 to 820
- probe_vector: float32 [128], replicated, may hold values from -4 to 4
Outputs:
- new_momentum: float32 [2, 2, 24, 6144, 128], P('grp', 'lay', None, 'col')
- update: float32 [2, 2, 24, 6144, 128], P('grp', 'lay', None, 'col')
All inputs are finite; a program needn't handle non-finite values.
Results may differ from a plain program's by a relative error of at most 0.00022.
Values sent between devices are 32-bit elements; how exact they have to be, the bound alone decides.
A program may use at most 128 MiB of HBM per device.

v0:
```python
import math

import jax
import jax.numpy as jnp
from jax import lax
from jax.sharding import PartitionSpec as P

D = 6144
ITERS = 3


MOMENTUM_DECAY = 0.95
LINEAR_TERM = 3.4445
CUBIC_TERM = -4.775
QUINTIC_TERM = 2.0315
EPSILON = 1e-06
PRECISE = lax.Precision.HIGHEST


def summed_gram(stack):
    partial_gram = jnp.einsum("glhdr,glhds->glhrs", stack, stack, precision=PRECISE)
    return lax.psum(partial_gram, "col")


def head_bound(product, probe_norm):
    estimate = jnp.sqrt(jnp.sum(product * product, axis=-1) + EPSILON) / probe_norm
    local_most = jnp.max(estimate, axis=(0, 1))
    overall = lax.pmax(local_most, ("grp", "lay"))
    return 2.0 * jnp.sqrt(overall)


def on_device(gradient, momentum, probe_vector):
    new_momentum = MOMENTUM_DECAY * momentum + gradient
    blend = gradient + MOMENTUM_DECAY * new_momentum
    width = blend.shape[-1]
    probe_norm = jnp.sqrt(jnp.sum(probe_vector * probe_vector) + EPSILON)
    raw_gram = summed_gram(blend)
    product = jnp.einsum("glhrs,s->glhr", raw_gram, probe_vector, precision=PRECISE)
    bound_value = head_bound(product, probe_norm)
    scaled = blend / bound_value[None, None, :, None, None]
    current = raw_gram / (bound_value * bound_value)[None, None, :, None, None]
    identity = jnp.eye(width, dtype=jnp.float32)
    total = jnp.broadcast_to(identity, current.shape)
    for counter in range(ITERS):
        square = jnp.einsum("glhrs,glhst->glhrt", current, current, precision=PRECISE)
        mixing = LINEAR_TERM * identity + CUBIC_TERM * current + QUINTIC_TERM * square
        total = jnp.einsum("glhrs,glhst->glhrt", total, mixing, precision=PRECISE)
        if counter + 1 < ITERS:
            halfway = jnp.einsum("glhrs,glhst->glhrt", mixing, current, precision=PRECISE)
            current = jnp.einsum("glhrs,glhst->glhrt", halfway, mixing, precision=PRECISE)
    polished = jnp.einsum("glhdr,glhrs->glhds", scaled, total, precision=PRECISE)
    update = polished * (0.2 * math.sqrt(D))
    return (new_momentum, update)


def solution(mesh):
    in_specs = (P("grp", "lay", None, "col", None), P("grp", "lay", None, "col", None), P())
    out_specs = (P("grp", "lay", None, "col", None), P("grp", "lay", None, "col", None))
    return jax.shard_map(
        on_device, mesh=mesh, in_specs=in_specs, out_specs=out_specs, check_vma=False
    )
```

profile of v0, /device:TPU:0, one launch (start us, length us, event | category | flops | bytes accessed | tf_op | source)
XLA Modules:
  0.0 162.3 jit_solution(10926613362764965501)
XLA Ops:
  7.2 0.0 all-reduce.2.cloned.1.call-start
  7.2 11.6 %multiply_add_fusion.1 = f32[1,1,24,768,128]{4,3,2,1,0:T(8,128)} fusion(f32[1,1,24,768,128]{4,3,2,1,0:T(8,128)} %param.3, f32[1,1,24,768,128]{4,3,2,1,0:T(8,128)} %param.4), kind=kLoop, calls=%fused_computation.7 | loop fusion | flops 4718592 | bytes 28311552 | tf_op jit(solution)/shard_map/add | solution.py:33
  18.8 29.0 %fusion.30 = f32[1,1,24,128,128]{4,3,2,1,0:T(8,128)} fusion(f32[1,1,24,768,128]{4,3,2,1,0:T(8,128)} %param.3, f32[1,1,24,768,128]{4,3,2,1,0:T(8,128)} %multiply_add_fusion.1), kind=kOutput, calls=%fused_computation.33 | convolution fusion | flops 3628597248 | bytes 20447232 | tf_op jit(solution)/shard_map/glhdr,glhds->glhrs/dot_general | solution.py:21
  47.8 0.0 copy-start.1
  47.8 0.0 all-reduce.2.cloned.1.call-update
  47.8 0.6 copy-done.1
  48.4 0.7 multiply_reduce_fusion.1
  49.8 62.7 %all-reduce.2.cloned.1.call-done = f32[1,1,24,128,128]{4,3,2,1,0:T(8,128)} async-done(((f32[1,1,24,128,128]{4,3,2,1,0:T(8,128)}), f32[1,1,24,128,128]{4,3,2,1,0:T(8,128)}) %all-reduce.2.cloned.1.call-update) | async-done | bytes 1572880 | tf_op jit(solution)/shard_map/psum | solution.py:22
  112.5 0.0 copy-start
  112.5 2.9 %fusion.17 = f32[1,24,128]{2,0,1:T(1,128)S(1)} fusion(f32[1,1,24,128,128]{4,3,2,1,0:T(8,128)} %all-reduce.2.cloned.1.call-done, f32[128]{0:T(128)S(1)} %copy-done.1), kind=kOutput, calls=%fused_computation.19 | convolution fusion | flops 4718592 | bytes 1585664 | tf_op jit(solution)/shard_map/glhrs,s->glhr/dot_general | solution.py:38
  115.5 0.1 multiply_reduce_fusion
  115.6 9.8 %pmax.7 = f32[24]{0:T(128)S(1)} all-reduce(f32[24]{0:T(128)S(1)} %sqrt_divide_fusion), channel_id=1, replica_groups=mesh['grp'=2,'col'=8,'lay'=2] {'grp','lay'}, use_global_device_ids=true, to_apply=%region_3.0 | all-reduce | flops 24 | bytes 192 | tf_op jit(solution)/shard_map/pmax | solution.py:28
  125.4 0.0 copy-done
  125.4 2.1 %bitcast_add_fusion = f32[1,1,24,128,128]{4,3,2,1,0:T(8,128)S(1)} fusion(f32[128,128]{1,0:T(8,128)S(1)} %fusion.48, f32[1,1,24,128,128]{4,3,2,1,0:T(8,128)S(1)} %copy-done, f32[24]{0:T(128)S(1)} %get-tuple-element.3), kind=kOutput, calls=%fused_computation.15 | convolution fusion | flops 606339072 | bytes 3211360 | tf_op jit(solution)/shard_map/glhrs,glhst->glhrt/dot_general | solution.py:45
  127.5 1.8 %fusion.10 = f32[24,128,128]{2,1,0:T(8,128)S(1)} fusion(f32[1,1,24,128,128]{4,3,2,1,0:T(8,128)S(1)} %bitcast_add_fusion, f32[1,1,24,128,128]{4,3,2,1,0:T(8,128)S(1)} %copy-done, f32[24]{0:T(128)S(1)} %get-tuple-element.3), kind=kOutput, calls=%fused_computation.11 | convolution fusion | flops 604372992 | bytes 4718688 | tf_op jit(solution)/shard_map/glhrs,glhst->glhrt/dot_general | solution.py:49
  129.3 1.7 %fusion.8 = f32[24,128,128]{2,1,0:T(8,128)S(1)} fusion(f32[24,128,128]{2,1,0:T(8,128)S(1)} %fusion.10, f32[1,1,24,128,128]{4,3,2,1,0:T(8,128)S(1)} %bitcast_add_fusion), kind=kOutput, calls=%fused_computation.9 | convolution fusion | flops 603979776 | bytes 4718592 | tf_op jit(solution)/shard_map/glhrs,glhst->glhrt/dot_general | solution.py:50
  131.0 0.0 slice-start.3
  131.0 1.6 fusion.12
  132.6 1.7 %fusion.62 = f32[24,128,128]{2,1,0:T(8,128)S(1)} fusion(f32[24,128,128]{2,1,0:T(8,128)S(1)} %fusion.8), kind=kOutput, calls=%fused_computation.67 | convolution fusion | flops 603979776 | bytes 3145728 | tf_op jit(solution)/shard_map/glhrs,glhst->glhrt/dot_general | solution.py:45
  134.3 0.0 slice-start.4
  134.3 1.9 %fusion.25 = f32[24,128,128]{2,1,0:T(8,128)S(1)} fusion(f32[24,128,128]{2,1,0:T(8,128)S(1)} %fusion.8, f32[24,128,128]{2,1,0:T(8,128)S(1)} %fusion.62, f32[128,128]{1,0:T(8,128)S(1)} %fusion.48), kind=kOutput, calls=%fused_computation.28 | convolution fusion | flops 605552640 | bytes 4784128 | tf_op jit(solution)/shard_map/glhrs,glhst->glhrt/dot_general | solution.py:49
  136.2 0.0 slice-start
  136.2 2.1 %fusion.26 = f32[24,128,128]{2,1,0:T(8,128)S(1)} fusion(f32[24,128,128]{2,1,0:T(8,128)S(1)} %fusion.12, f32[24,128,128]{2,1,0:T(8,128)S(1)} %fusion.62, f32[24,128,128]{2,1,0:T(8,128)S(1)} %fusion.8, f32[128,128]{1,0:T(8,128)S(1)} %fusion.48), kind=kOutput, calls=%fused_computation.29 | convolution fusion | flops 605552640 | bytes 6356992 | tf_op jit(solution)/shard_map/glhrs,glhst->glhrt/dot_general | solution.py:47
  138.3 0.0 slice-start.1
  138.4 0.0 slice-start.5
  138.4 1.9 %fusion.24 = f32[24,128,128]{2,1,0:T(8,128)S(1)} fusion(f32[24,128,128]{2,1,0:T(8,128)S(1)} %fusion.25, f32[24,128,128]{2,1,0:T(8,128)S(1)} %fusion.62, f32[24,128,128]{2,1,0:T(8,128)S(1)} %fusion.8, f32[128,128]{1,0:T(8,128)S(1)} %fusion.48), kind=kOutput, calls=%fused_computation.27 | convolution fusion | flops 605552640 | bytes 6356992 | tf_op jit(solution)/shard_map/glhrs,glhst->glhrt/dot_general | solution.py:50
  140.2 0.0 slice-start.2
  140.3 1.7 %fusion.63 = f32[24,128,128]{2,1,0:T(8,128)S(1)} fusion(f32[24,128,128]{2,1,0:T(8,128)S(1)} %fusion.24), kind=kOutput, calls=%fused_computation.68 | convolution fusion | flops 603979776 | bytes 3145728 | tf_op jit(solution)/shard_map/glhrs,glhst->glhrt/dot_general | solution.py:45
  141.9 1.9 %fusion.19 = f32[24,128,128]{2,1,0:T(8,128)S(1)} fusion(f32[24,128,128]{2,1,0:T(8,128)S(1)} %fusion.26, f32[24,128,128]{2,1,0:T(8,128)S(1)} %fusion.63, f32[24,128,128]{2,1,0:T(8,128)S(1)} %fusion.24, f32[128,128]{1,0:T(8,128)S(1)} %fusion.48), kind=kOutput, calls=%fused_computation.21 | convolution fusion | flops 605552640 | bytes 6356992 | tf_op jit(solution)/shard_map/glhrs,glhst->glhrt/dot_general | solution.py:47
  143.8 0.0 slice-done.3
  143.8 0.0 slice-done.4
  143.8 0.0 slice-done
  143.8 0.0 slice-done.1
  143.8 0.0 slice-done.5
  143.9 0.0 slice-done.2
  143.9 11.6 %multiply_bitcast_fusion = f32[1,1,24,768,128]{4,3,2,1,0:T(8,128)} fusion(f32[24,128,128]{2,1,0:T(8,128)S(1)} %fusion.19, f32[24]{0:T(128)S(1)} %get-tuple-element.2, f32[1,1,24,768,128]{4,3,2,1,0:T(8,128)S(1)} %bitcast.49, f32[1,1,24,768,128]{4,3,2,1,0:T(8,128)S(1)} %bitcast.51), kind=kOutput, calls=%fused_computation.4 | convolution fusion | flops 3633315840 | bytes 29884512 | tf_op jit(solution)/shard_map/glhdr,glhrs->glhds/dot_general | solution.py:51
  (6 shorter events, 0.0 us)
Async XLA Ops:
  7.2 105.4 %all-reduce.2.cloned.1.call-start = ((), (), s32[]{:S(2)}) async-start(), calls=%async_computation | async-start | bytes 3145728 | tf_op jit(solution)/shard_map/psum | solution.py:22
  47.8 0.7 copy-start.1
  112.5 12.9 %copy-start = (f32[1,1,24,128,128]{4,3,2,1,0:T(8,128)S(1)}, f32[1,1,24,128,128]{4,3,2,1,0:T(8,128)}, u32[]{:S(2)}) copy-start(f32[1,1,24,128,128]{4,3,2,1,0:T(8,128)} %all-reduce.2.cloned.1.call-done) | copy-start | bytes 4718596
  131.0 12.8 %slice-start.3 = ((s8[9437184]{0:T(1024)(128)(4,1)}), s8[4194304]{0:T(1024)(128)(4,1)S(1)}, s32[]{:S(2)}) async-start(s8[9437184]{0:T(1024)(128)(4,1)} %bitcast.50), calls=%async_computation.4 | async-start | bytes 8388608
  134.3 9.5 %slice-start.4 = ((s8[9437184]{0:T(1024)(128)(4,1)}), s8[4194304]{0:T(1024)(128)(4,1)S(1)}, s32[]{:S(2)}) async-start(s8[9437184]{0:T(1024)(128)(4,1)} %bitcast.50), calls=%async_computation.5 | async-start | bytes 8388608
  136.2 7.6 %slice-start = ((s8[9437184]{0:T(1024)(128)(4,1)}), s8[4194304]{0:T(1024)(128)(4,1)S(1)}, s32[]{:S(2)}) async-start(s8[9437184]{0:T(1024)(128)(4,1)} %bitcast.48), calls=%async_computation.1 | async-start | bytes 8388608
  138.3 5.5 %slice-start.1 = ((s8[9437184]{0:T(1024)(128)(4,1)}), s8[4194304]{0:T(1024)(128)(4,1)S(1)}, s32[]{:S(2)}) async-start(s8[9437184]{0:T(1024)(128)(4,1)} %bitcast.48), calls=%async_computation.2 | async-start | bytes 8388608
  138.4 5.5 %slice-start.5 = ((s8[9437184]{0:T(1024)(128)(4,1)}), s8[1048576]{0:T(1024)(128)(4,1)S(1)}, s32[]{:S(2)}) async-start(s8[9437184]{0:T(1024)(128)(4,1)} %bitcast.50), calls=%async_computation.6 | async-start | bytes 2097152
  140.2 3.6 %slice-start.2 = ((s8[9437184]{0:T(1024)(128)(4,1)}), s8[1048576]{0:T(1024)(128)(4,1)S(1)}, s32[]{:S(2)}) async-start(s8[9437184]{0:T(1024)(128)(4,1)} %bitcast.48), calls=%async_computation.3 | async-start | bytes 2097152
Sparse Core Ops, SparseCore 0:
  47.9 64.5 all-reduce.1
where the time goes:
time: 162 us
  waiting for transfers between devices  62.7 us (39%)
  matrix products  61.7 us (38%)
  between operations  14.9 us (9%)
  other arithmetic  12.4 us (8%)
  blocking collectives  9.78 us (6%)
    psum x1, waiting for transfers between devices, summed_gram(): return lax.psum(partial_gram, 'col')  62.7 us
    dot_general x1, matrix products, summed_gram(): jnp.einsum('glhdr,glhds->glhrs', stack, stack, precision=PRECISE)  29 us
    add x1, other arithmetic, on_device(): new_momentum = MOMENTUM_DECAY * momentum + gradient  11.6 us
    dot_general x1, matrix products, on_device(): jnp.einsum('glhdr,glhrs->glhds', scaled, total, precision=PRECISE)  11.6 us
    pmax x1, blocking collectives, head_bound(): overall = lax.pmax(local_most, ('grp', 'lay'))  9.78 us
    dot_general x3, matrix products, on_device(): total = jnp.einsum('glhrs,glhst->glhrt', total, mixing, precision=PRECISE)  5.55 us
    dot_general x3, matrix products, on_device(): jnp.einsum('glhrs,glhst->glhrt', current, current, precision=PRECISE)  5.4 us
    dot_general x2, matrix products, on_device(): jnp.einsum('glhrs,glhst->glhrt', mixing, current, precision=PRECISE)  3.67 us
  transfers between devices with their start and end apart: 1, of which 1 were waited for; matrix products, arithmetic and copies ran while one was open for 0% of the time, Pallas kernels for 0%

commit v1 on v0

--- a/solution.py
+++ b/solution.py
@@ -1,8 +1,11 @@
+import functools
 import math
 
 import jax
 import jax.numpy as jnp
 from jax import lax
+from jax.experimental import pallas as pl
+from jax.experimental.pallas import tpu as pltpu
 from jax.sharding import PartitionSpec as P
 
 D = 6144
@@ -15,6 +18,341 @@
 QUINTIC_TERM = 2.0315
 EPSILON = 1e-06
 PRECISE = lax.Precision.HIGHEST
+MESH = pl.DeviceIdType.MESH
+CORES = 2
+PAD = 8
+
+
+def split(x):
+    high = x.astype(jnp.bfloat16)
+    low = (x - high.astype(jnp.float32)).astype(jnp.bfloat16)
+    return high, low
+
+
+def weights(w):
+    high, low = split(w)
+    top = jnp.concatenate([high, low], axis=1)
+    bottom = jnp.concatenate([high, jnp.zeros_like(high)], axis=1)
+    return jnp.concatenate([top, bottom], axis=0)
+
+
+def matmul(x, w_cat):
+    n = x.shape[1]
+    both = jnp.concatenate(split(x), axis=1)
+    out = jnp.dot(both, w_cat, preferred_element_type=jnp.float32)
+    return out[:, :n] + out[:, n:]
+
+
+def places(half, width):
+    row = lax.broadcasted_iota(jnp.int32, (half, width), 0)
+    lane = lax.broadcasted_iota(jnp.int32, (half, width), 1)
+    return row, lane
+
+
+def pack(sym):
+    width = sym.shape[0]
+    half = width // 2
+    row, lane = places(half, width)
+    top, bottom = sym[:half], sym[half:]
+    body = jnp.where(lane >= row, top, pltpu.roll(bottom, half, 1))
+    diagonal = jnp.sum(jnp.where(lane == row + half, bottom, 0.0), axis=0, keepdims=True)
+    return body, jnp.broadcast_to(diagonal, (PAD, width))
+
+
+def unpack(body, diagonal):
+    half, width = body.shape
+    row, lane = places(half, width)
+    top = jnp.where(lane > row, body, jnp.where(lane == row, 0.5 * body, 0.0))
+    rolled = pltpu.roll(body, half, 1)
+    bottom = jnp.where((lane >= half) & (lane < row + half), rolled, 0.0)
+    bottom = bottom + jnp.where(lane == row + half, 0.5 * diagonal, 0.0)
+    tri = jnp.concatenate([top, bottom], axis=0)
+    return tri + tri.T
+
+
+def gram_kernel(gradient, momentum, new_momentum, blend, gram):
+    heads, rows, width = blend.shape
+    half = width // 2
+
+    def body(g_ref, m_ref, n_ref):
+        h = pl.program_id(0)
+        g = g_ref[0]
+        fresh = MOMENTUM_DECAY * m_ref[0] + g
+        n_ref[0] = fresh
+        y = g + MOMENTUM_DECAY * fresh
+        blend[h] = y
+        high, low = split(y)
+        both = jnp.concatenate([high, low], axis=1)
+        out = lax.dot_general(
+            high, both, (((0,), (0,)), ((), ())), preferred_element_type=jnp.float32
+        )
+        cross = out[:, width:]
+        packed, diagonal = pack(out[:, :width] + cross + cross.T)
+        gram[h, :half] = packed
+        gram[h, half:] = diagonal
+
+    block = pl.BlockSpec((1, rows, width), lambda h: (h, 0, 0))
+    pltpu.emit_pipeline(body, grid=(heads,), in_specs=[block, block], out_specs=[block])(
+        gradient, momentum, new_momentum
+    )
+
+
+def polish_kernel(sizes, scale, gram, probe, total, sib, acc, up_in, down_in, mine,
+                  est_out, est_in, got,
+                  sib_send, sib_recv, up_sems, down_sems, est_send, est_recv,
+                  out_up, out_down, pair_send, pair_recv):
+    n_grp, n_col, n_lay = sizes
+    ring = n_col // CORES
+    per = gram.shape[1]
+    width = gram.shape[3]
+    half = width // 2
+    up, down = ring // 2, (ring - 1) // 2
+    grp, col, lay = lax.axis_index("grp"), lax.axis_index("col"), lax.axis_index("lay")
+    z, core = col // CORES, lax.rem(col, CORES)
+    way = 1 - 2 * core
+
+    def chip(offset):
+        return lax.rem(z + offset + CORES * ring, ring)
+
+    def at(offset, c=core):
+        return chip(offset) * CORES + c
+
+    other = 1 - core
+    partner = at(0, other)
+    ahead, behind = at(way), at(-way)
+    peer_count = n_grp * n_lay
+    me = grp * n_lay + lay
+
+    def peer(t):
+        index = lax.rem(me + t, peer_count)
+        return {"grp": index // n_lay, "lay": lax.rem(index, n_lay)}
+
+    neighbours = [{"col": partner}]
+    if ring > 1:
+        neighbours.append({"col": ahead})
+    if ring > 2:
+        neighbours.append({"col": behind})
+    neighbours += [peer(t) for t in range(1, peer_count)]
+    barrier = pltpu.get_barrier_semaphore()
+    for neighbour in neighbours:
+        pl.semaphore_signal(barrier, inc=1, device_id=neighbour, device_id_type=MESH)
+    pl.semaphore_wait(barrier, len(neighbours))
+
+    def send(src, dst, s_sem, r_sem, device):
+        return pltpu.make_async_remote_copy(
+            src_ref=src, dst_ref=dst, send_sem=s_sem, recv_sem=r_sem,
+            device_id=device, device_id_type=MESH,
+        )
+
+    offsets = []
+    for s in range(max(up, down)):
+        if s < up:
+            offsets.append(up - s)
+        if s < down:
+            offsets.append(-(down - s))
+    offsets.append(0)
+    slot = {o: j for j, o in enumerate(offsets)}
+
+    pair = []
+    for j, o in enumerate(offsets):
+        copy = send(gram.at[at(-way * o, other)], sib.at[j], sib_send.at[j], sib_recv.at[j],
+                    {"col": partner})
+        copy.start()
+        pair.append(copy)
+
+    def join(o):
+        j = slot[o]
+        pair[j].wait_recv()
+        return gram[at(way * o)] + sib[j]
+
+    flights = []
+    flows = []
+    for steps, sign, inbox, sems, target in (
+        (up, 1, up_in, up_sems, ahead), (down, -1, down_in, down_sems, behind)
+    ):
+        flows.append((steps, sign, inbox, sems, target, []))
+    for s in range(max(up, down)):
+        for steps, sign, inbox, sems, target, copies in flows:
+            if s >= steps:
+                continue
+            o = sign * (steps - s)
+            j = slot[o]
+            value = join(o)
+            if s:
+                copies[s - 1].wait_recv()
+                value = value + inbox[s - 1]
+            acc[j] = value
+            copy = send(acc.at[j], inbox.at[s], sems.at[0, s], sems.at[1, s], {"col": target})
+            copy.start()
+            copies.append(copy)
+            flights.append(copy)
+    value = join(0)
+    for steps, sign, inbox, sems, target, copies in flows:
+        if steps:
+            copies[steps - 1].wait_recv()
+            value = value + inbox[steps - 1]
+    mine[...] = value
+
+    probe_row = probe[0:1, :]
+    probe_norm = jnp.sqrt(jnp.sum(probe_row * probe_row, keepdims=True) + EPSILON)
+    grams = []
+    for i in range(per):
+        full = unpack(mine[i, :half], mine[i, half:half + 1])
+        grams.append(full)
+        product = jnp.sum(full * probe_row, axis=1, keepdims=True)
+        estimate = jnp.sqrt(jnp.sum(product * product, keepdims=True) + EPSILON) / probe_norm
+        est_out[i] = jnp.broadcast_to(estimate, (PAD, width))
+    shares = []
+    for t in range(1, peer_count):
+        copy = send(est_out, est_in.at[t - 1], est_send.at[t - 1], est_recv.at[t - 1], peer(t))
+        copy.start()
+        shares.append(copy)
+    for copy in shares:
+        copy.wait_recv()
+    row, lane = places(width, width)
+    identity = jnp.where(row == lane, 1.0, 0.0)
+    currents, totals, bounds = [], [], []
+    for i in range(per):
+        most = est_out[i, 0:1]
+        for t in range(1, peer_count):
+            most = jnp.maximum(most, est_in[t - 1, i, 0:1])
+        bound = 2.0 * jnp.sqrt(most)
+        bounds.append(bound)
+        currents.append(grams[i] / (bound * bound))
+        totals.append(None)
+    for counter in range(ITERS):
+        cats = [weights(c) for c in currents]
+        squares = [matmul(c, w) for c, w in zip(currents, cats)]
+        mixing = [
+            LINEAR_TERM * identity + CUBIC_TERM * c + QUINTIC_TERM * s
+            for c, s in zip(currents, squares)
+        ]
+        mixed = [weights(m) for m in mixing]
+        if counter + 1 < ITERS:
+            halfway = [matmul(m, w) for m, w in zip(mixing, cats)]
+        totals = [m if t is None else matmul(t, w) for t, m, w in zip(totals, mixing, mixed)]
+        if counter + 1 < ITERS:
+            currents = [matmul(h, w) for h, w in zip(halfway, mixed)]
+    for i in range(per):
+        body, diagonal = pack(totals[i] * (scale / bounds[i]))
+        got[col, i, :half] = body
+        got[col, i, half:] = diagonal
+
+    def spread(index, position):
+        copy = send(got.at[index], got.at[index], pair_send.at[position],
+                    pair_recv.at[position], {"col": partner})
+        copy.start()
+        flights.append(copy)
+
+    def pass_on(s, sign, sems, target):
+        index = at(-way * sign * s)
+        copy = send(got.at[index], got.at[index], sems.at[0, s], sems.at[1, s], {"col": target})
+        copy.start()
+        flights.append(copy)
+
+    def arrived(index, s_sem, r_sem):
+        send(got.at[index], got.at[index], s_sem, r_sem, {"col": partner}).wait_recv()
+
+    def unfold(index):
+        for i in range(per):
+            total[index * per + i] = unpack(got[index, i, :half], got[index, i, half:half + 1])
+
+    if up:
+        pass_on(0, 1, out_up, ahead)
+    if down:
+        pass_on(0, -1, out_down, behind)
+    spread(col, 0)
+    unfold(col)
+    order = [0]
+    for s in range(max(up, down)):
+        for steps, sign, sems, target in ((up, 1, out_up, ahead), (down, -1, out_down, behind)):
+            if s >= steps:
+                continue
+            o = -sign * (s + 1)
+            index = at(way * o)
+            arrived(index, sems.at[0, s], sems.at[1, s])
+            if s + 1 < steps:
+                pass_on(s + 1, sign, sems, target)
+            spread(index, len(order))
+            order.append(o)
+            unfold(index)
+    for position, o in enumerate(order):
+        index = at(-way * o, other)
+        arrived(index, pair_send.at[position], pair_recv.at[position])
+        unfold(index)
+    for copy in pair + flights + shares:
+        copy.wait_send()
+
+
+def apply_kernel(blend, total, update):
+    heads, rows, width = blend.shape
+
+    def body(u_ref):
+        h = pl.program_id(0)
+        u_ref[0] = matmul(blend[h], weights(total[h]))
+
+    block = pl.BlockSpec((1, rows, width), lambda h: (h, 0, 0))
+    pltpu.emit_pipeline(body, grid=(heads,), in_specs=[], out_specs=[block])(update)
+
+
+def on_device_kernels(sizes, gradient, momentum, probe_vector):
+    n_grp, n_col, n_lay = sizes
+    _, _, heads, rows, width = gradient.shape
+    per, ring = heads // n_col, n_col // CORES
+    depth = width // 2 + PAD
+    up, down = ring // 2, (ring - 1) // 2
+    peers = max(n_grp * n_lay - 1, 1)
+    f32 = jnp.float32
+    any_spec, vmem_spec = pl.BlockSpec(memory_space=pl.ANY), pl.BlockSpec(memory_space=pltpu.VMEM)
+    limit = 24 * 1024 * 1024
+    new_momentum, blend, gram = pl.pallas_call(
+        gram_kernel,
+        out_shape=(
+            jax.ShapeDtypeStruct((heads, rows, width), f32),
+            pltpu.VMEM((heads, rows, width), f32),
+            pltpu.VMEM((heads, depth, width), f32),
+        ),
+        in_specs=[any_spec, any_spec],
+        out_specs=(any_spec, vmem_spec, vmem_spec),
+        compiler_params=pltpu.CompilerParams(vmem_limit_bytes=limit),
+        name="gram",
+    )(gradient.reshape(heads, rows, width), momentum.reshape(heads, rows, width))
+    chunk = (per, depth, width)
+    dma = pltpu.SemaphoreType.DMA
+    total = pl.pallas_call(
+        functools.partial(polish_kernel, sizes, 0.2 * math.sqrt(rows * n_col)),
+        out_shape=pltpu.VMEM((heads, width, width), f32),
+        in_specs=[vmem_spec, vmem_spec],
+        out_specs=vmem_spec,
+        scratch_shapes=[
+            pltpu.VMEM((ring,) + chunk, f32),
+            pltpu.VMEM((ring,) + chunk, f32),
+            pltpu.VMEM((max(up, 1),) + chunk, f32),
+            pltpu.VMEM((max(down, 1),) + chunk, f32),
+            pltpu.VMEM(chunk, f32),
+            pltpu.VMEM((per, PAD, width), f32),
+            pltpu.VMEM((peers, per, PAD, width), f32),
+            pltpu.VMEM((n_col,) + chunk, f32),
+            dma((ring,)), dma((ring,)),
+            dma((2, max(up, 1))), dma((2, max(down, 1))),
+            dma((peers,)), dma((peers,)),
+            dma((2, max(up, 1))), dma((2, max(down, 1))),
+            dma((ring,)), dma((ring,)),
+        ],
+        compiler_params=pltpu.CompilerParams(
+            collective_id=0, has_side_effects=True, vmem_limit_bytes=limit
+        ),
+        name="polish",
+    )(gram.reshape((n_col,) + chunk), probe_vector.reshape(1, width))
+    update = pl.pallas_call(
+        apply_kernel,
+        out_shape=jax.ShapeDtypeStruct((heads, rows, width), f32),
+        in_specs=[vmem_spec, vmem_spec],
+        out_specs=any_spec,
+        compiler_params=pltpu.CompilerParams(vmem_limit_bytes=limit),
+        name="apply",
+    )(blend, total)
+    return new_momentum.reshape(gradient.shape), update.reshape(gradient.shape)
 
 
 def summed_gram(stack):
@@ -54,8 +392,17 @@
 
 
 def solution(mesh):
+    sizes = (mesh.shape["grp"], mesh.shape["col"], mesh.shape["lay"])
+
+    def local(gradient, momentum, probe_vector):
+        heads = gradient.shape[2]
+        whole_heads = heads % sizes[1] == 0 and sizes[1] % CORES == 0
+        if whole_heads and gradient.shape[:2] == (1, 1):
+            return on_device_kernels(sizes, gradient, momentum, probe_vector)
+        return on_device(gradient, momentum, probe_vector)
+
     in_specs = (P("grp", "lay", None, "col", None), P("grp", "lay", None, "col", None), P())
     out_specs = (P("grp", "lay", None, "col", None), P("grp", "lay", None, "col", None))
     return jax.shard_map(
-        on_device, mesh=mesh, in_specs=in_specs, out_specs=out_specs, check_vma=False
+        local, mesh=mesh, in_specs=in_specs, out_specs=out_specs, check_vma=False
     )

time: 162 us -> 71.9 us (0.44)
  Pallas kernels: 0 us -> 63.6 us
  waiting for transfers between devices: 62.7 us -> 0 us
  matrix products: 61.7 us -> 0 us
  between operations: 14.9 us -> 0.65 us
  other arithmetic: 12.4 us -> 0 us
  blocking collectives: 9.78 us -> 0 us
  local copies, waits for them, and re-layouts: 0.68 us -> 7.36 us
    pallas_call x0 -> x3, Pallas kernels: none -> 63.6 us  [the longest x1 31.4 us: on_device_kernels(): pl.pallas_call(functools.partial(polish_kernel, sizes, 0.2 * math.sqrt(ro...]
    psum x1 -> x0, waiting for transfers between devices: 62.7 us -> none  [summed_gram(): return lax.psum(partial_gram, 'col')]
    dot_general x13 -> x0, matrix products: 61.7 us -> none  [the longest x1 29 us: summed_gram(): jnp.einsum('glhdr,glhds->glhrs', stack, stack, precision=PRECISE)]
    add x1 -> x0, other arithmetic: 11.6 us -> none  [on_device(): new_momentum = MOMENTUM_DECAY * momentum + gradient]
    pmax x1 -> x0, blocking collectives: 9.78 us -> none  [head_bound(): overall = lax.pmax(local_most, ('grp', 'lay'))]
    unnamed x16 -> x6, local copies, waits for them, and re-layouts: 0.68 us -> 7.36 us
  transfers between devices with their start and end apart: 1 -> 0, of which waited for: 1 -> 0; matrix products, arithmetic and copies ran while one was open for 0% -> 0% of each run, Pallas kernels for 0% -> 0%
where the time goes in v1:
time: 71.9 us; the launch traced here: 71.7 us
  Pallas kernels  63.6 us (88%)
  local copies, waits for them, and re-layouts  7.36 us (10%)
    pallas_call x1, Pallas kernels, on_device_kernels(): pl.pallas_call(functools.partial(polish_kernel, sizes, 0.2 * math.sqrt(ro...  31.4 us
    pallas_call x1, Pallas kernels, on_device_kernels(): pl.pallas_call(gram_kernel, out_shape=(jax.ShapeDtypeStruct((heads, rows,...  19.7 us
    pallas_call x1, Pallas kernels, on_device_kernels(): pl.pallas_call(apply_kernel, out_shape=jax.ShapeDtypeStruct((heads, rows,...  12.5 us
    unnamed x6, local copies, waits for them, and re-layouts  7.36 us

profile of v1, /device:TPU:0, one launch (start us, length us, event | category | flops | bytes accessed | tf_op | source)
XLA Modules:
  0.0 71.7 jit_solution(14509819993568667770)
XLA Ops:
  0.6 0.0 copy-start
  0.6 3.7 %copy-done = f32[1,1,24,768,128]{4,3,2,1,0:T(8,128)S(1)} copy-done((f32[1,1,24,768,128]{4,3,2,1,0:T(8,128)S(1)}, f32[1,1,24,768,128]{4,3,2,1,0:T(8,128)}, u32[]{:S(2)}) %copy-start) | copy-done | bytes 9437208
  4.3 0.0 copy-start.1
  4.3 3.7 %copy-done.1 = f32[1,1,24,768,128]{4,3,2,1,0:T(8,128)S(1)} copy-done((f32[1,1,24,768,128]{4,3,2,1,0:T(8,128)S(1)}, f32[1,1,24,768,128]{4,3,2,1,0:T(8,128)}, u32[]{:S(2)}) %copy-start.1) | copy-done | bytes 9437208
  8.0 0.0 copy-start.2
  8.0 19.7 %gram.1 = (f32[24,768,128]{2,1,0:T(8,128)}, f32[24,768,128]{2,1,0:T(8,128)S(1)}, f32[24,72,128]{2,1,0:T(8,128)S(1)}) custom-call(f32[24,768,128]{2,1,0:T(8,128)S(1)} %bitcast.6, f32[24,768,128]{2,1,0:T(8,128)S(1)} %bitcast.7), custom_call_target="tpu_custom_call" | custom-call | tf_op jit(solution)/shard_map/gram/pallas_call | solution.py:308
  27.7 0.0 copy-done.2
  27.7 31.4 %polish.1.total = f32[24,128,128]{2,1,0:T(8,128)S(1)} custom-call(f32[8,3,72,128]{3,2,1,0:T(8,128)S(1)} %bitcast.8, f32[1,128]{1,0:T(1,128)S(1)} %bitcast.9), custom_call_target="tpu_custom_call" | custom-call | tf_op jit(solution)/shard_map/polish/pallas_call | solution.py:322
  59.1 12.5 %apply.1 = f32[24,768,128]{2,1,0:T(8,128)} custom-call(f32[24,768,128]{2,1,0:T(8,128)S(1)} %get-tuple-element.6.blend, f32[24,128,128]{2,1,0:T(8,128)S(1)} %polish.1.total), custom_call_target="tpu_custom_call" | custom-call | tf_op jit(solution)/shard_map/apply/pallas_call | solution.py:347
Async XLA Ops:
  0.6 3.7 %copy-start = (f32[1,1,24,768,128]{4,3,2,1,0:T(8,128)S(1)}, f32[1,1,24,768,128]{4,3,2,1,0:T(8,128)}, u32[]{:S(2)}) copy-start(f32[1,1,24,768,128]{4,3,2,1,0:T(8,128)} %param.3) | copy-start | bytes 28311556
  4.3 3.7 %copy-start.1 = (f32[1,1,24,768,128]{4,3,2,1,0:T(8,128)S(1)}, f32[1,1,24,768,128]{4,3,2,1,0:T(8,128)}, u32[]{:S(2)}) copy-start(f32[1,1,24,768,128]{4,3,2,1,0:T(8,128)} %param.4) | copy-start | bytes 28311556
  8.0 19.7 %copy-start.2 = (f32[128]{0:T(128)S(1)}, f32[128]{0:T(128)}, u32[]{:S(2)}) copy-start(f32[128]{0:T(128)} %param.5) | copy-start | bytes 1540

commit v2 on v1

--- a/solution.py
+++ b/solution.py
@@ -21,6 +21,7 @@
 MESH = pl.DeviceIdType.MESH
 CORES = 2
 PAD = 8
+BUFFERS = 3
 
 
 def split(x):
@@ -70,35 +71,9 @@
     return tri + tri.T
 
 
-def gram_kernel(gradient, momentum, new_momentum, blend, gram):
-    heads, rows, width = blend.shape
-    half = width // 2
-
-    def body(g_ref, m_ref, n_ref):
-        h = pl.program_id(0)
-        g = g_ref[0]
-        fresh = MOMENTUM_DECAY * m_ref[0] + g
-        n_ref[0] = fresh
-        y = g + MOMENTUM_DECAY * fresh
-        blend[h] = y
-        high, low = split(y)
-        both = jnp.concatenate([high, low], axis=1)
-        out = lax.dot_general(
-            high, both, (((0,), (0,)), ((), ())), preferred_element_type=jnp.float32
-        )
-        cross = out[:, width:]
-        packed, diagonal = pack(out[:, :width] + cross + cross.T)
-        gram[h, :half] = packed
-        gram[h, half:] = diagonal
-
-    block = pl.BlockSpec((1, rows, width), lambda h: (h, 0, 0))
-    pltpu.emit_pipeline(body, grid=(heads,), in_specs=[block, block], out_specs=[block])(
-        gradient, momentum, new_momentum
-    )
-
-
-def polish_kernel(sizes, scale, gram, probe, total, sib, acc, up_in, down_in, mine,
-                  est_out, est_in, got,
+def polish_kernel(sizes, scale, gradient, momentum, probe, new_momentum, blend, total,
+                  g_in, m_in, gram, sib, acc, up_in, down_in, mine,
+                  est_out, est_in, got, g_sem, m_sem,
                   sib_send, sib_recv, up_sems, down_sems, est_send, est_recv,
                   out_up, out_down, pair_send, pair_recv):
     n_grp, n_col, n_lay = sizes
@@ -106,6 +81,7 @@
     per = gram.shape[1]
     width = gram.shape[3]
     half = width // 2
+    depth = g_in.shape[0]
     up, down = ring // 2, (ring - 1) // 2
     grp, col, lay = lax.axis_index("grp"), lax.axis_index("col"), lax.axis_index("lay")
     z, core = col // CORES, lax.rem(col, CORES)
@@ -136,7 +112,6 @@
     barrier = pltpu.get_barrier_semaphore()
     for neighbour in neighbours:
         pl.semaphore_signal(barrier, inc=1, device_id=neighbour, device_id_type=MESH)
-    pl.semaphore_wait(barrier, len(neighbours))
 
     def send(src, dst, s_sem, r_sem, device):
         return pltpu.make_async_remote_copy(
@@ -153,46 +128,91 @@
     offsets.append(0)
     slot = {o: j for j, o in enumerate(offsets)}
 
-    pair = []
-    for j, o in enumerate(offsets):
-        copy = send(gram.at[at(-way * o, other)], sib.at[j], sib_send.at[j], sib_recv.at[j],
-                    {"col": partner})
-        copy.start()
-        pair.append(copy)
-
-    def join(o):
-        j = slot[o]
-        pair[j].wait_recv()
-        return gram[at(way * o)] + sib[j]
+    def offset_of(j):
+        return sum(o * jnp.where(j == i, 1, 0) for i, o in enumerate(offsets) if o)
+
+    def owner(t):
+        own = lax.rem(t, 2)
+        place = chip((2 * own - 1) * way * offset_of(t // 2))
+        return place * CORES + lax.rem(core + 1 + own, CORES)
+
+    def loads(t):
+        heads = pl.ds(owner(t) * per, per)
+        b = lax.rem(t, depth)
+        return (
+            pltpu.make_async_copy(gradient.at[heads], g_in.at[b], g_sem.at[b]),
+            pltpu.make_async_copy(momentum.at[heads], m_in.at[b], m_sem.at[b]),
+        )
+
+    def pair_copy(j):
+        return send(gram.at[at(-way * offsets[j], other)], sib.at[j],
+                    sib_send.at[j], sib_recv.at[j], {"col": partner})
+
+    flows = ((up, 1, up_in, up_sems, ahead), (down, -1, down_in, down_sems, behind))
+
+    def flow_copy(flow, s):
+        steps, sign, inbox, sems, target = flow
+        return send(acc.at[slot[sign * (steps - s)]], inbox.at[s],
+                    sems.at[0, s], sems.at[1, s], {"col": target})
+
+    hops = []
+    for s in range(max(up, down)):
+        hops += [(flow, s) for flow in flows if s < flow[0]]
+
+    def join(j):
+        pair_copy(j).wait_recv()
+        value = gram[at(way * offsets[j])] + sib[j]
+        if j + 1 == ring:
+            for flow in flows:
+                if flow[0]:
+                    flow_copy(flow, flow[0] - 1).wait_recv()
+                    value = value + flow[2][flow[0] - 1]
+            mine[...] = value
+            return
+        flow, s = hops[j]
+        if s:
+            flow_copy(flow, s - 1).wait_recv()
+            value = value + flow[2][s - 1]
+        acc[j] = value
+        flow_copy(flow, s).start()
+
+    steps = 2 * ring
+    for t in range(min(depth - 1, steps)):
+        for copy in loads(t):
+            copy.start()
+
+    pl.semaphore_wait(barrier, len(neighbours))
+
+    @pl.loop(0, steps)
+    def _(t):
+        @pl.when(t + depth - 1 < steps)
+        def _():
+            for copy in loads(t + depth - 1):
+                copy.start()
+
+        for copy in loads(t):
+            copy.wait()
+        index, b = owner(t), lax.rem(t, depth)
+        for i in range(per):
+            h = index * per + i
+            g = g_in[b, i]
+            fresh = MOMENTUM_DECAY * m_in[b, i] + g
+            new_momentum[h] = fresh
+            high, low = split(g + MOMENTUM_DECAY * fresh)
+            both = jnp.concatenate([high, low], axis=1)
+            blend[h] = both
+            out = lax.dot_general(
+                high, both, (((0,), (0,)), ((), ())), preferred_element_type=jnp.float32
+            )
+            cross = out[:, width:]
+            packed, diagonal = pack(out[:, :width] + cross + cross.T)
+            gram[index, i, :half] = packed
+            gram[index, i, half:] = diagonal
+        for j in range(ring):
+            pl.when(t == 2 * j)(lambda j=j: pair_copy(j).start())
+            pl.when(t == 2 * j + 1)(functools.partial(join, j))
 
     flights = []
-    flows = []
-    for steps, sign, inbox, sems, target in (
-        (up, 1, up_in, up_sems, ahead), (down, -1, down_in, down_sems, behind)
-    ):
-        flows.append((steps, sign, inbox, sems, target, []))
-    for s in range(max(up, down)):
-        for steps, sign, inbox, sems, target, copies in flows:
-            if s >= steps:
-                continue
-            o = sign * (steps - s)
-            j = slot[o]
-            value = join(o)
-            if s:
-                copies[s - 1].wait_recv()
-                value = value + inbox[s - 1]
-            acc[j] = value
-            copy = send(acc.at[j], inbox.at[s], sems.at[0, s], sems.at[1, s], {"col": target})
-            copy.start()
-            copies.append(copy)
-            flights.append(copy)
-    value = join(0)
-    for steps, sign, inbox, sems, target, copies in flows:
-        if steps:
-            copies[steps - 1].wait_recv()
-            value = value + inbox[steps - 1]
-    mine[...] = value
-
     probe_row = probe[0:1, :]
     probe_norm = jnp.sqrt(jnp.sum(probe_row * probe_row, keepdims=True) + EPSILON)
     grams = []
@@ -255,7 +275,8 @@
 
     def unfold(index):
         for i in range(per):
-            total[index * per + i] = unpack(got[index, i, :half], got[index, i, half:half + 1])
+            full = unpack(got[index, i, :half], got[index, i, half:half + 1])
+            total[index * per + i] = weights(full)
 
     if up:
         pass_on(0, 1, out_up, ahead)
@@ -280,19 +301,29 @@
         index = at(-way * o, other)
         arrived(index, pair_send.at[position], pair_recv.at[position])
         unfold(index)
-    for copy in pair + flights + shares:
+    for j in range(ring):
+        pair_copy(j).wait_send()
+    for flow, s in hops:
+        flow_copy(flow, s).wait_send()
+    for copy in flights + shares:
         copy.wait_send()
 
 
-def apply_kernel(blend, total, update):
-    heads, rows, width = blend.shape
+def apply_kernel(per, fresh, blend, total, new_momentum, update, sem):
+    heads, rows, width = fresh.shape
+    copy = pltpu.make_async_copy(fresh, new_momentum, sem)
+    copy.start()
 
     def body(u_ref):
-        h = pl.program_id(0)
-        u_ref[0] = matmul(blend[h], weights(total[h]))
-
-    block = pl.BlockSpec((1, rows, width), lambda h: (h, 0, 0))
-    pltpu.emit_pipeline(body, grid=(heads,), in_specs=[], out_specs=[block])(update)
+        step = pl.program_id(0)
+        for i in range(per):
+            h = step * per + i
+            out = jnp.dot(blend[h], total[h], preferred_element_type=jnp.float32)
+            u_ref[i] = out[:, :width] + out[:, width:]
+
+    block = pl.BlockSpec((per, rows, width), lambda s: (s, 0, 0))
+    pltpu.emit_pipeline(body, grid=(heads // per,), in_specs=[], out_specs=[block])(update)
+    copy.wait()
 
 
 def on_device_kernels(sizes, gradient, momentum, probe_vector):
@@ -302,29 +333,24 @@
     depth = width // 2 + PAD
     up, down = ring // 2, (ring - 1) // 2
     peers = max(n_grp * n_lay - 1, 1)
-    f32 = jnp.float32
+    f32, bf16 = jnp.float32, jnp.bfloat16
     any_spec, vmem_spec = pl.BlockSpec(memory_space=pl.ANY), pl.BlockSpec(memory_space=pltpu.VMEM)
     limit = 24 * 1024 * 1024
-    new_momentum, blend, gram = pl.pallas_call(
-        gram_kernel,
-        out_shape=(
-            jax.ShapeDtypeStruct((heads, rows, width), f32),
-            pltpu.VMEM((heads, rows, width), f32),
-            pltpu.VMEM((heads, depth, width), f32),
-        ),
-        in_specs=[any_spec, any_spec],
-        out_specs=(any_spec, vmem_spec, vmem_spec),
-        compiler_params=pltpu.CompilerParams(vmem_limit_bytes=limit),
-        name="gram",
-    )(gradient.reshape(heads, rows, width), momentum.reshape(heads, rows, width))
     chunk = (per, depth, width)
     dma = pltpu.SemaphoreType.DMA
-    total = pl.pallas_call(
+    fresh, blend, total = pl.pallas_call(
         functools.partial(polish_kernel, sizes, 0.2 * math.sqrt(rows * n_col)),
-        out_shape=pltpu.VMEM((heads, width, width), f32),
-        in_specs=[vmem_spec, vmem_spec],
-        out_specs=vmem_spec,
+        out_shape=(
+            pltpu.VMEM((heads, rows, width), f32),
+            pltpu.VMEM((heads, rows, 2 * width), bf16),
+            pltpu.VMEM((heads, 2 * width, 2 * width), bf16),
+        ),
+        in_specs=[any_spec, any_spec, vmem_spec],
+        out_specs=(vmem_spec, vmem_spec, vmem_spec),
         scratch_shapes=[
+            pltpu.VMEM((BUFFERS, per, rows, width), f32),
+            pltpu.VMEM((BUFFERS, per, rows, width), f32),
+            pltpu.VMEM((n_col,) + chunk, f32),
             pltpu.VMEM((ring,) + chunk, f32),
             pltpu.VMEM((ring,) + chunk, f32),
             pltpu.VMEM((max(up, 1),) + chunk, f32),
@@ -333,6 +359,7 @@
             pltpu.VMEM((per, PAD, width), f32),
             pltpu.VMEM((peers, per, PAD, width), f32),
             pltpu.VMEM((n_col,) + chunk, f32),
+            dma((BUFFERS,)), dma((BUFFERS,)),
             dma((ring,)), dma((ring,)),
             dma((2, max(up, 1))), dma((2, max(down, 1))),
             dma((peers,)), dma((peers,)),
@@ -343,15 +370,20 @@
             collective_id=0, has_side_effects=True, vmem_limit_bytes=limit
         ),
         name="polish",
-    )(gram.reshape((n_col,) + chunk), probe_vector.reshape(1, width))
-    update = pl.pallas_call(
-        apply_kernel,
-        out_shape=jax.ShapeDtypeStruct((heads, rows, width), f32),
-        in_specs=[vmem_spec, vmem_spec],
-        out_specs=any_spec,
+    )(
+        pltpu.with_memory_space_constraint(gradient.reshape(heads, rows, width), pltpu.HBM),
+        pltpu.with_memory_space_constraint(momentum.reshape(heads, rows, width), pltpu.HBM),
+        probe_vector.reshape(1, width),
+    )
+    new_momentum, update = pl.pallas_call(
+        functools.partial(apply_kernel, per),
+        out_shape=(jax.ShapeDtypeStruct((heads, rows, width), f32),) * 2,
+        in_specs=[vmem_spec, vmem_spec, vmem_spec],
+        out_specs=(any_spec, any_spec),
+        scratch_shapes=[dma],
         compiler_params=pltpu.CompilerParams(vmem_limit_bytes=limit),
         name="apply",
-    )(blend, total)
+    )(fresh, blend, total)
     return new_momentum.reshape(gradient.shape), update.reshape(gradient.shape)
 
 

time: 71.9 us -> 42.9 us (0.60)
  Pallas kernels: 63.6 us -> 41.4 us
  local copies, waits for them, and re-layouts: 7.36 us -> 0.65 us
    pallas_call x2 -> x1, Pallas kernels: 32.2 us -> 9.06 us  [on_device_kernels(): pl.pallas_call(functools.partial(apply_kernel, per), out_shape=(jax.Shape...]
    unnamed x6 -> x2, local copies, waits for them, and re-layouts: 7.36 us -> 0.65 us
    pallas_call x1, Pallas kernels: 31.4 us -> 32.3 us  [on_device_kernels(): pl.pallas_call(functools.partial(polish_kernel, sizes, 0.2 * math.sqrt(ro...]
where the time goes in v2:
time: 42.9 us; the launch traced here: 42.7 us
  Pallas kernels  41.4 us (97%)
  local copies, waits for them, and re-layouts  0.65 us (2%)
  between operations  0.65 us (2%)
    pallas_call x1, Pallas kernels, on_device_kernels(): pl.pallas_call(functools.partial(polish_kernel, sizes, 0.2 * math.sqrt(ro...  32.3 us
    pallas_call x1, Pallas kernels, on_device_kernels(): pl.pallas_call(functools.partial(apply_kernel, per), out_shape=(jax.Shape...  9.06 us

profile of v2, /device:TPU:0, one launch (start us, length us, event | category | flops | bytes accessed | tf_op | source)
XLA Modules:
  0.0 42.7 jit_solution(13610147539234064257)
XLA Ops:
  0.6 0.0 copy-start
  0.6 0.6 %copy-done = f32[128]{0:T(128)S(1)} copy-done((f32[128]{0:T(128)S(1)}, f32[128]{0:T(128)}, u32[]{:S(2)}) %copy-start) | copy-done | bytes 536
  1.3 32.3 %polish.1 = (f32[24,768,128]{2,1,0:T(8,128)S(1)}, bf16[24,768,256]{2,1,0:T(8,128)(2,1)S(1)}, bf16[24,256,256]{2,1,0:T(8,128)(2,1)S(1)}) custom-call(f32[24,768,128]{2,1,0:T(8,128)} %bitcast.6, f32[24,768,128]{2,1,0:T(8,128)} %bitcast.7, f32[1,128]{1,0:T(1,128)S(1)} %bitcast.5), custom_call_target="tpu_custom_call" | custom-call | tf_op jit(solution)/shard_map/polish/pallas_call | solution.py:341
  33.6 9.1 %apply.1 = (f32[24,768,128]{2,1,0:T(8,128)}, f32[24,768,128]{2,1,0:T(8,128)}) custom-call(f32[24,768,128]{2,1,0:T(8,128)S(1)} %get-tuple-element.7.fresh, bf16[24,768,256]{2,1,0:T(8,128)(2,1)S(1)} %get-tuple-element.8.blend, bf16[24,256,256]{2,1,0:T(8,128)(2,1)S(1)} %get-tuple-element.9.total), custom_call_target="tpu_custom_call" | custom-call | tf_op jit(solution)/shard_map/apply/pallas_call | solution.py:378
Async XLA Ops:
  0.6 0.7 %copy-start = (f32[128]{0:T(128)S(1)}, f32[128]{0:T(128)}, u32[]{:S(2)}) copy-start(f32[128]{0:T(128)} %param.5) | copy-start | bytes 1540
